TPU v7x, 32 devices: a whole 2x2x4 slice. The times are simulated.
32 devices in a mesh: phase: 4 (over y, x), line: 8 (over z, core).
Axes of the slice: x: 2, y: 2, z: 4, core: 2. Of those that a mesh axis runs over, the one named last changes fastest.
Arguments:
- signal: bfloat16 [4, 8, 8192, 256], P('phase', 'line'), may hold values from -8 to 8, as said below
- tap_gain: float32 [3, 256], replicated, may hold values from 0.3 to 1.2
Outputs:
- echoed: bfloat16 [4, 8, 8192, 256], P('phase', 'line')
Inputs may be any that keep to these rules, and one draw needn't show every extreme that they name: signal holds numbers from -8 to 8.
All inputs are finite; a program needn't handle non-finite values.
Results may differ from a plain program's by a relative error of at most 0.0055.
Values may be sent and summed in bfloat16 or wider, within the bound.
A program may use at most 64 MiB of HBM per device.

v0:
```python
import jax
import jax.numpy as jnp
from jax import lax
from jax.sharding import PartitionSpec as P


def from_behind(block, axis, distance):
    devices = range(lax.axis_size(axis))
    route = [((i - distance) % len(devices), i) for i in devices]
    return lax.ppermute(block, axis, route)


def per_device(signal, tap_gain):
    wide_in = signal.astype(jnp.float32)
    copy_1 = from_behind(signal, "phase", 2)
    copy_2 = from_behind(signal, "phase", 3)
    mixed = (
        tap_gain[0] * wide_in
        + tap_gain[1] * copy_1.astype(jnp.float32)
        + tap_gain[2] * copy_2.astype(jnp.float32)
    )
    power = lax.psum(jnp.sum(mixed * mixed, axis=(0, 2), keepdims=True), "phase") / (
        signal.shape[2] * lax.axis_size("phase")
    )
    echoed = (mixed * lax.rsqrt(power + 1e-05)).astype(jnp.bfloat16)
    return echoed


def solution(mesh):
    return jax.shard_map(
        per_device,
        mesh=mesh,
        in_specs=(P("phase", "line", None, None), P()),
        out_specs=P("phase", "line", None, None),
        check_vma=False,
    )
```

profile of v0, /device:TPU:0, one launch (start us, length us, event | category | flops | bytes accessed | tf_op | source)
XLA Modules:
  0.0 207.1 jit_solution(7272801855755148704)
XLA Ops:
  0.0 4.0 %collective-permute-start.1 = (bf16[1,1,8192,256]{3,2,1,0:T(8,128)(2,1)}, bf16[1,1,8192,256]{3,2,1,0:T(8,128)(2,1)S(1)}, u32[]{:S(2)}, u32[]{:S(2)}) collective-permute-start(bf16[1,1,8192,256]{3,2,1,0:T(8,128)(2,1)} %param.2), channel_id=1, source_target_pairs={{8,0},{16,8},{24,16},{0,24},{9,1},{17,9},{25,17},{1,25},{10,2},{18... | collective-permute-start | bytes 12582920 | tf_op jit(solution)/shard_map/ppermute | solution.py:10
  4.0 0.5 collective-permute-start
  4.5 0.8 fusion
  5.3 89.3 %collective-permute-done.1 = bf16[1,1,8192,256]{3,2,1,0:T(8,128)(2,1)S(1)} collective-permute-done((bf16[1,1,8192,256]{3,2,1,0:T(8,128)(2,1)}, bf16[1,1,8192,256]{3,2,1,0:T(8,128)(2,1)S(1)}, u32[]{:S(2)}, u32[]{:S(2)}) %collective-permute-start.1) | collective-permute-done | bytes 4194336 | tf_op jit(solution)/shard_map/ppermute | solution.py:10
  94.6 0.0 copy-start
  94.6 1.6 collective-permute-done
  96.2 0.0 copy-start.1
  96.2 5.7 %multiply_reduce_fusion = f32[256]{0:T(256)S(1)} fusion(bf16[1,1,8192,256]{3,2,1,0:T(8,128)(2,1)S(1)} %collective-permute-done.1, f32[256]{0:T(256)S(1)} %bitcast.7, bf16[1,1,8192,256]{3,2,1,0:T(8,128)(2,1)S(1)} %collective-permute-done, f32[256]{0:T(256)S(1)} %bitcast.9, bf16[1,1,8192,256]{3,2,1,0:T(8,128)(2,1)} %param.2, f32[256]{0:T(256)S(1)} %bitcast.5), kind=kLoop, calls=%fused_computation.1 | loop fusion | flops 20971264 | bytes 12587008 | tf_op jit(solution)/shard_map/reduce_sum | solution.py:22
  101.9 0.0 copy-done
  101.9 0.0 copy-done.1
  101.9 97.8 %psum.7 = f32[1,1,1,256]{3,2,1,0:T(1,128)S(1)} all-reduce(f32[1,1,1,256]{3,2,1,0:T(1,128)S(1)} %bitcast.12), channel_id=1, replica_groups=mesh['phase'=4,'line'=8] {'phase'}, use_global_device_ids=true, to_apply=%region_1.0 | all-reduce | flops 256 | bytes 2048 | tf_op jit(solution)/shard_map/psum | solution.py:22
  199.7 7.3 %multiply_convert_fusion = bf16[1,1,8192,256]{3,2,1,0:T(8,128)(2,1)} fusion(f32[256]{0:T(256)S(1)} %bitcast.11, bf16[1,1,8192,256]{3,2,1,0:T(8,128)(2,1)} %copy-done, f32[256]{0:T(256)S(1)} %bitcast.8, bf16[1,1,8192,256]{3,2,1,0:T(8,128)(2,1)} %copy-done.1, f32[256]{0:T(256)S(1)} %bitcast.10, bf16[1,1,8192,256]{3,2,1,0:T(8,128)(2,1)} %param.2, f32[256]{0:T(256)S(1)} %bitcast.6), kind=kLoop, calls=%fused_computation | loop fusion | flops 20971520 | bytes 16781312 | tf_op jit(solution)/shard_map/convert_element_type | solution.py:25
  (1 shorter events, 0.0 us)
Async XLA Ops:
  0.0 94.6 %collective-permute-start.1 = (bf16[1,1,8192,256]{3,2,1,0:T(8,128)(2,1)}, bf16[1,1,8192,256]{3,2,1,0:T(8,128)(2,1)S(1)}, u32[]{:S(2)}, u32[]{:S(2)}) collective-permute-start(bf16[1,1,8192,256]{3,2,1,0:T(8,128)(2,1)} %param.2), channel_id=1, source_target_pairs={{8,0},{16,8},{24,16},{0,24},{9,1},{17,9},{25,17},{1,25},{10,2},{18... | collective-permute-start | bytes 12582920 | tf_op jit(solution)/shard_map/ppermute | solution.py:10
  4.0 92.2 %collective-permute-start = (bf16[1,1,8192,256]{3,2,1,0:T(8,128)(2,1)}, bf16[1,1,8192,256]{3,2,1,0:T(8,128)(2,1)S(1)}, u32[]{:S(2)}, u32[]{:S(2)}) collective-permute-start(bf16[1,1,8192,256]{3,2,1,0:T(8,128)(2,1)} %param.2), channel_id=1, source_target_pairs={{16,0},{24,8},{0,16},{8,24},{17,1},{25,9},{1,17},{9,25},{18,2},{26... | collective-permute-start | bytes 12582920 | tf_op jit(solution)/shard_map/ppermute | solution.py:10
  94.6 7.4 %copy-start = (bf16[1,1,8192,256]{3,2,1,0:T(8,128)(2,1)}, bf16[1,1,8192,256]{3,2,1,0:T(8,128)(2,1)S(1)}, u32[]{:S(2)}) copy-start(bf16[1,1,8192,256]{3,2,1,0:T(8,128)(2,1)S(1)} %collective-permute-done.1) | copy-start | bytes 12582916
  96.2 5.7 %copy-start.1 = (bf16[1,1,8192,256]{3,2,1,0:T(8,128)(2,1)}, bf16[1,1,8192,256]{3,2,1,0:T(8,128)(2,1)S(1)}, u32[]{:S(2)}) copy-start(bf16[1,1,8192,256]{3,2,1,0:T(8,128)(2,1)S(1)} %collective-permute-done) | copy-start | bytes 12582916
where the time goes:
time: 207 us
  blocking collectives  97.8 us (47%)
  waiting for transfers between devices  90.9 us (44%)
  other arithmetic  13.1 us (6%)
  starting transfers between devices  4.46 us (2%)
    psum x1, blocking collectives, per_device(): lax.psum(jnp.sum(mixed * mixed, axis=(0, 2), keepdims=True), 'phase')  97.8 us
    ppermute x2, waiting for transfers between devices, from_behind(): return lax.ppermute(block, axis, route)  90.9 us
    convert_element_type x1, other arithmetic, per_device(): echoed = (mixed * lax.rsqrt(power + 1e-05)).astype(jnp.bfloat16)  7.34 us
    reduce_sum x1, other arithmetic, per_device(): jnp.sum(mixed * mixed, axis=(0, 2), keepdims=True)  5.72 us
    ppermute x2, starting transfers between devices, from_behind(): return lax.ppermute(block, axis, route)  4.46 us
  transfers between devices with their start and end apart: 2, of which 2 were waited for; matrix products, arithmetic and copies ran while one was open for 0% of the time, Pallas kernels for 0%

commit v1 on v0

v1 whole, which is shorter than its diff:
```python
import functools

import jax
import jax.numpy as jnp
from jax import lax
from jax.experimental import pallas as pl
from jax.experimental.pallas import tpu as pltpu
from jax.sharding import PartitionSpec as P

MESH = pl.DeviceIdType.MESH
CHUNK_ROWS = 256
LAG = 2
SUB_ROWS = 64
STORE_ROWS = 512


def exchange_kernel(
    n, chunk, signal_ref, gain_ref, mixed_ref, scale_ref,
    near, far, sums, load_sem, out1_sem, in1_sem, out2_sem, in2_sem, sum_out, sum_in,
):
    me = lax.axis_index("phase")
    rows = near.shape[1]
    steps = rows // chunk
    to_1 = lax.rem(me + 2, n)
    if n == 4:
        odd = lax.rem(me, 2)
        to_2 = me + 1 - 2 * odd
        held = 1 - odd
    else:
        to_2 = lax.rem(me + 3, n)
        held = 0

    def part(k):
        return pl.ds(pl.multiple_of(k * chunk, chunk), chunk)

    def load(k):
        return pltpu.make_async_copy(
            signal_ref.at[0, 0, part(k)], near.at[0, part(k)], load_sem.at[k]
        )

    def send_1(k):
        return pltpu.make_async_remote_copy(
            src_ref=near.at[0, part(k)], dst_ref=near.at[1, part(k)],
            send_sem=out1_sem.at[k], recv_sem=in1_sem.at[k],
            device_id={"phase": to_1}, device_id_type=MESH,
        )

    def send_2(k):
        return pltpu.make_async_remote_copy(
            src_ref=near.at[held, part(k)], dst_ref=far.at[part(k)],
            send_sem=out2_sem.at[k], recv_sem=in2_sem.at[k],
            device_id={"phase": to_2}, device_id_type=MESH,
        )

    def send_sum(d):
        return pltpu.make_async_remote_copy(
            src_ref=sums.at[0], dst_ref=sums.at[d],
            send_sem=sum_out.at[d], recv_sem=sum_in.at[d],
            device_id={"phase": lax.rem(me + d, n)}, device_id_type=MESH,
        )

    def each(body):
        lax.fori_loop(0, steps, lambda k, c: (body(k), c)[1], 0)

    each(lambda k: load(k).start())
    barrier = pltpu.get_barrier_semaphore()
    for d in range(1, n):
        pl.semaphore_signal(
            barrier, inc=1, device_id={"phase": lax.rem(me + d, n)}, device_id_type=MESH
        )
    pl.semaphore_wait(barrier, n - 1)

    def first(k):
        load(k).wait()
        send_1(k).start()

    each(first)

    g0, g1, g2 = (gain_ref[pl.ds(i, 1), :] for i in range(3))

    def mix(k, total):
        send_2(k).wait_recv()
        for j in range(chunk // SUB_ROWS):
            at = pl.ds(pl.multiple_of(k * chunk + j * SUB_ROWS, SUB_ROWS), SUB_ROWS)
            mixed = (
                g0 * near[0, at, :].astype(jnp.float32)
                + g1 * near[1, at, :].astype(jnp.float32)
                + g2 * far[at, :].astype(jnp.float32)
            )
            mixed_ref[at, :] = mixed
            total = total + jnp.sum((mixed * mixed).reshape(SUB_ROWS // 8, 8, -1), axis=0)
        return total

    def pass_on(k):
        send_1(k).wait_recv()
        send_2(k).start()

    def step(k, total):
        pass_on(k)
        return mix(k - LAG, total)

    lax.fori_loop(0, LAG, lambda k, c: (pass_on(k), c)[1], 0)
    total = lax.fori_loop(LAG, steps, step, jnp.zeros(sums.shape[1:], jnp.float32))
    total = lax.fori_loop(steps - LAG, steps, mix, total)

    sums[0] = total
    for d in range(1, n):
        send_sum(d).start()
    for d in range(1, n):
        send_sum(d).wait_recv()
    for d in range(1, n):
        total = total + sums[d]
    power = jnp.sum(total, axis=0, keepdims=True) * (1.0 / (rows * n))
    scale_ref[...] = lax.rsqrt(power + 1e-5)

    def last(k):
        send_1(k).wait_send()
        send_2(k).wait_send()

    each(last)
    for d in range(1, n):
        send_sum(d).wait_send()


def scale_kernel(mixed_ref, scale_ref, out_ref):
    size = out_ref.shape[2]
    start = pl.multiple_of(pl.program_id(0) * size, size)
    out_ref[0, 0] = (mixed_ref[pl.ds(start, size), :] * scale_ref[...]).astype(out_ref.dtype)


def per_device(n, signal, tap_gain):
    _, _, rows, channels = signal.shape
    chunk = CHUNK_ROWS
    while rows % chunk:
        chunk //= 2
    steps = rows // chunk
    vmem = pl.BlockSpec(memory_space=pltpu.VMEM)
    dma = pltpu.SemaphoreType.DMA
    mixed, scale = pl.pallas_call(
        functools.partial(exchange_kernel, n, chunk),
        out_shape=(
            pltpu.VMEM((rows, channels), jnp.float32),
            pltpu.VMEM((1, channels), jnp.float32),
        ),
        in_specs=[pl.BlockSpec(memory_space=pltpu.HBM), vmem],
        out_specs=(vmem, vmem),
        scratch_shapes=[
            pltpu.VMEM((2, rows, channels), signal.dtype),
            pltpu.VMEM((rows, channels), signal.dtype),
            pltpu.VMEM((n, 8, channels), jnp.float32),
            dma((steps,)), dma((steps,)), dma((steps,)), dma((steps,)), dma((steps,)),
            dma((n,)), dma((n,)),
        ],
        compiler_params=pltpu.CompilerParams(
            collective_id=0, has_side_effects=True, vmem_limit_bytes=32 * 2**20
        ),
        name="exchange",
    )(signal, tap_gain)
    size = min(STORE_ROWS, rows)
    return pl.pallas_call(
        scale_kernel,
        grid=(rows // size,),
        out_shape=jax.ShapeDtypeStruct(signal.shape, jnp.bfloat16),
        in_specs=[vmem, vmem],
        out_specs=pl.BlockSpec((1, 1, size, channels), lambda i: (0, 0, i, 0)),
        compiler_params=pltpu.CompilerParams(vmem_limit_bytes=16 * 2**20),
        name="rescale",
    )(mixed, scale)


def solution(mesh):
    return jax.shard_map(
        functools.partial(per_device, mesh.shape["phase"]),
        mesh=mesh,
        in_specs=(P("phase", "line", None, None), P()),
        out_specs=P("phase", "line", None, None),
        check_vma=False,
    )
```

time: 207 us -> 120 us (0.58)
  Pallas kernels: 0 us -> 117 us
  blocking collectives: 97.8 us -> 0 us
  waiting for transfers between devices: 90.9 us -> 0 us
  other arithmetic: 13.1 us -> 0 us
  starting transfers between devices: 4.46 us -> 0 us
    pallas_call x0 -> x2, Pallas kernels: none -> 117 us  [the longest x1 111 us: per_device(): pl.pallas_call(functools.partial(exchange_kernel, n, chunk), out_shape=(p...]
    psum x1 -> x0, blocking collectives: 97.8 us -> none  [per_device(): lax.psum(jnp.sum(mixed * mixed, axis=(0, 2), keepdims=True), 'phase')]
    ppermute x2 -> x0, waiting for transfers between devices: 90.9 us -> none  [from_behind(): return lax.ppermute(block, axis, route)]
    convert_element_type x1 -> x0, other arithmetic: 7.34 us -> none  [per_device(): echoed = (mixed * lax.rsqrt(power + 1e-05)).astype(jnp.bfloat16)]
    reduce_sum x1 -> x0, other arithmetic: 5.72 us -> none  [per_device(): jnp.sum(mixed * mixed, axis=(0, 2), keepdims=True)]
    ppermute x2 -> x0, starting transfers between devices: 4.46 us -> none  [from_behind(): return lax.ppermute(block, axis, route)]
    unnamed x4, local copies, waits for them, and re-layouts: 0.01 us -> 2.87 us
  transfers between devices with their start and end apart: 2 -> 0, of which waited for: 2 -> 0; matrix products, arithmetic and copies ran while one was open for 0% -> 0% of each run, Pallas kernels for 0% -> 0%
where the time goes in v1:
time: 120 us
  Pallas kernels  117 us (98%)
  local copies, waits for them, and re-layouts  2.87 us (2%)
    pallas_call x1, Pallas kernels, per_device(): pl.pallas_call(functools.partial(exchange_kernel, n, chunk), out_shape=(p...  111 us
    pallas_call x1, Pallas kernels, per_device(): pl.pallas_call(scale_kernel, grid=(rows // size,), out_shape=jax.ShapeDty...  5.96 us
    unnamed x4, local copies, waits for them, and re-layouts  2.87 us

profile of v1, /device:TPU:0, one launch (start us, length us, event | category | flops | bytes accessed | tf_op | source)
XLA Modules:
  0.0 119.6 jit_solution(10789423289872414466)
XLA Ops:
  0.0 0.0 copy-start
  0.0 2.2 %copy-done = bf16[1,1,8192,256]{3,2,1,0:T(8,128)(2,1)S(1)} copy-done((bf16[1,1,8192,256]{3,2,1,0:T(8,128)(2,1)S(1)}, bf16[1,1,8192,256]{3,2,1,0:T(8,128)(2,1)}, u32[]{:S(2)}) %copy-start) | copy-done | bytes 4194328
  2.2 0.0 copy-start.1
  2.2 0.7 copy-done.1
  2.9 110.8 %exchange.1 = (f32[8192,256]{1,0:T(8,128)S(1)}, f32[1,256]{1,0:T(1,128)S(1)}) custom-call(bf16[1,1,8192,256]{3,2,1,0:T(8,128)(2,1)S(1)} %copy-done, f32[3,256]{1,0:T(4,128)S(1)} %copy-done.1), custom_call_target="tpu_custom_call" | custom-call | tf_op jit(solution)/shard_map/exchange/pallas_call | solution.py:139
  113.7 6.0 %rescale.1 = bf16[1,1,8192,256]{3,2,1,0:T(8,128)(2,1)} custom-call(f32[8192,256]{1,0:T(8,128)S(1)} %get-tuple-element.7.mixed_ref, f32[1,256]{1,0:T(1,128)S(1)} %get-tuple-element.8.scale_ref), custom_call_target="tpu_custom_call" | custom-call | tf_op jit(solution)/shard_map/rescale/pallas_call | solution.py:160
Async XLA Ops:
  0.0 2.2 %copy-start = (bf16[1,1,8192,256]{3,2,1,0:T(8,128)(2,1)S(1)}, bf16[1,1,8192,256]{3,2,1,0:T(8,128)(2,1)}, u32[]{:S(2)}) copy-start(bf16[1,1,8192,256]{3,2,1,0:T(8,128)(2,1)} %signal_ref.1) | copy-start | bytes 12582916
  2.2 0.7 copy-start.1

commit v2 on v1

--- a/solution.py
+++ b/solution.py
@@ -11,7 +11,7 @@
 CHUNK_ROWS = 256
 LAG = 2
 SUB_ROWS = 64
-STORE_ROWS = 512
+STORE_ROWS = 1024
 
 
 def exchange_kernel(
@@ -122,10 +122,27 @@
         send_sum(d).wait_send()
 
 
-def scale_kernel(mixed_ref, scale_ref, out_ref):
-    size = out_ref.shape[2]
-    start = pl.multiple_of(pl.program_id(0) * size, size)
-    out_ref[0, 0] = (mixed_ref[pl.ds(start, size), :] * scale_ref[...]).astype(out_ref.dtype)
+def scale_kernel(size, mixed_ref, scale_ref, out_ref, held, sem):
+    def store(k):
+        at = pl.ds(pl.multiple_of(k * size, size), size)
+        return pltpu.make_async_copy(held.at[at], out_ref.at[0, 0, at], sem.at[k])
+
+    scale = scale_ref[...]
+
+    def step(k, c):
+        for j in range(size // SUB_ROWS):
+            at = pl.ds(pl.multiple_of(k * size + j * SUB_ROWS, SUB_ROWS), SUB_ROWS)
+            held[at, :] = (mixed_ref[at, :] * scale).astype(held.dtype)
+        store(k).start()
+        return c
+
+    def finish(k, c):
+        store(k).wait()
+        return c
+
+    blocks = held.shape[0] // size
+    lax.fori_loop(0, blocks, step, 0)
+    lax.fori_loop(0, blocks, finish, 0)
 
 
 def per_device(n, signal, tap_gain):
@@ -152,17 +169,22 @@
             dma((n,)), dma((n,)),
         ],
         compiler_params=pltpu.CompilerParams(
-            collective_id=0, has_side_effects=True, vmem_limit_bytes=32 * 2**20
+            collective_id=0, has_side_effects=True, vmem_limit_bytes=54 * 2**20
         ),
         name="exchange",
     )(signal, tap_gain)
-    size = min(STORE_ROWS, rows)
+    size = STORE_ROWS
+    while rows % size:
+        size //= 2
     return pl.pallas_call(
-        scale_kernel,
-        grid=(rows // size,),
+        functools.partial(scale_kernel, size),
         out_shape=jax.ShapeDtypeStruct(signal.shape, jnp.bfloat16),
         in_specs=[vmem, vmem],
-        out_specs=pl.BlockSpec((1, 1, size, channels), lambda i: (0, 0, i, 0)),
+        out_specs=pl.BlockSpec(memory_space=pltpu.HBM),
+        scratch_shapes=[
+            pltpu.VMEM((rows, channels), jnp.bfloat16),
+            dma((rows // size,)),
+        ],
         compiler_params=pltpu.CompilerParams(vmem_limit_bytes=16 * 2**20),
         name="rescale",
     )(mixed, scale)

time: 120 us -> 108 us (0.900)
  Pallas kernels: 117 us -> 108 us
  local copies, waits for them, and re-layouts: 2.87 us -> 0 us
    pallas_call x1, Pallas kernels: 111 us -> 106 us  [per_device(): pl.pallas_call(functools.partial(exchange_kernel, n, chunk), out_shape=(p...]
    pallas_call x1, Pallas kernels: 5.96 us -> 2.17 us  [per_device(): pl.pallas_call(functools.partial(scale_kernel, size), out_shape=jax.Shape...]
    unnamed x4 -> x0, local copies, waits for them, and re-layouts: 2.87 us -> none
where the time goes in v2:
time: 108 us
  Pallas kernels  108 us (100%)
    pallas_call x1, Pallas kernels, per_device(): pl.pallas_call(functools.partial(exchange_kernel, n, chunk), out_shape=(p...  106 us
    pallas_call x1, Pallas kernels, per_device(): pl.pallas_call(functools.partial(scale_kernel, size), out_shape=jax.Shape...  2.17 us

profile of v2, /device:TPU:0, one launch (start us, length us, event | category | flops | bytes accessed | tf_op | source)
XLA Modules:
  0.0 108.2 jit_solution(11841086316952871046)
XLA Ops:
  0.0 106.1 %exchange.1 = (f32[8192,256]{1,0:T(8,128)S(1)}, f32[1,256]{1,0:T(1,128)S(1)}) custom-call(bf16[1,1,8192,256]{3,2,1,0:T(8,128)(2,1)} %signal_ref.1, f32[3,256]{1,0:T(4,128)} %gain_ref.1), custom_call_target="tpu_custom_call" | custom-call | tf_op jit(solution)/shard_map/exchange/pallas_call | solution.py:156
  106.1 2.2 %rescale.1 = bf16[1,1,8192,256]{3,2,1,0:T(8,128)(2,1)} custom-call(f32[8192,256]{1,0:T(8,128)S(1)} %get-tuple-element.7.mixed_ref, f32[1,256]{1,0:T(1,128)S(1)} %get-tuple-element.8.scale_ref), custom_call_target="tpu_custom_call" | custom-call | tf_op jit(solution)/shard_map/rescale/pallas_call | solution.py:179
